TPU v7x, 32 devices: a whole 2x2x4 slice. The times are simulated.
32 devices in a mesh: row: 4 (over z), col: 8 (over y, x, core).
Axes of the slice: x: 2, y: 2, z: 4, core: 2. Of those that a mesh axis runs over, the one named last changes fastest.
Arguments:
- rhs: float32 [64, 131072], P(None, ('row', 'col')), may hold values from -6 to 6
- pivots: int32 [4096], replicated, may hold values from 0 to 131071, as said below
- factor: float32 [4096, 4, 8, 128], P('row', None, 'col'), as said below
- diag_inv: float32 [8, 512, 512], P('row'), as said below
Outputs:
- solution: float32 [64, 4, 8, 128], P(None, None, 'col')
Inputs may be any that keep to these rules, and one draw needn't show every extreme that they name: `pivots`: distinct column numbers, the first 4096 entries of a permutation of 0 .. 131071. `factor`: entry (row i, column q) is zero where q >= 512 * (i // 512). `diag_inv`: each block is unit lower triangular.
All inputs are finite; a program needn't handle non-finite values.
Results may differ from a plain program's by a relative error of at most 0.0001.
Values sent between devices are 32-bit elements; how exact they have to be, the bound alone decides.
A program may use at most 64 MiB of HBM per device.

v0:
```python
import jax
import jax.numpy as jnp
from jax import lax
from jax.sharding import PartitionSpec as P


def broadcast(shard, axis, root):
    mine = lax.axis_index(axis) == root
    return lax.psum(jnp.where(mine, shard, jnp.zeros_like(shard)), axis)


def apply_inverse(values, block_inv):
    return lax.dot_general(
        values,
        block_inv,
        (((1,), (1,)), ((), ())),
        precision=lax.Precision.HIGHEST,
        preferred_element_type=jnp.float32,
    )


def per_device(rhs, pivots, factor, diag_inv):
    my_row = lax.axis_index("row")
    my_col = lax.axis_index("col")
    col_count = lax.axis_size("col")
    rhs_count = rhs.shape[0]
    slab_rows = factor.shape[0]
    rounds = factor.shape[1]
    piece_len = factor.shape[3]
    block_len = diag_inv.shape[1]
    pieces = block_len // piece_len
    blocks_here = slab_rows // block_len
    total_blocks = blocks_here * lax.axis_size("row")
    first_column = (my_row * col_count + my_col) * rhs.shape[1]
    source_len = rhs.shape[1]
    located = pivots - first_column
    inside = (located >= 0) & (located < source_len)
    taken = jnp.take(rhs, jnp.clip(located, 0, source_len - 1), axis=1)
    taken = jnp.where(inside[None, :], taken, 0.0)
    permuted = lax.psum_scatter(
        jnp.transpose(
            taken.reshape(rhs_count, blocks_here * lax.axis_size("row"), block_len), (1, 0, 2)
        ),
        "row",
        scatter_dimension=0,
        tiled=True,
    )
    permuted = lax.psum(permuted, "col")
    factor_rows = factor.reshape(slab_rows, rounds * piece_len)

    def advance(number, solved):
        owner_row = number // blocks_here
        local_block = number % blocks_here
        block_rows = lax.dynamic_slice_in_dim(factor_rows, local_block * block_len, block_len, 0)
        partial_value = lax.dot_general(
            solved.reshape(rhs_count, rounds * piece_len),
            block_rows,
            (((1,), (1,)), ((), ())),
            precision=lax.Precision.HIGHEST,
            preferred_element_type=jnp.float32,
        )
        own_rhs = lax.dynamic_index_in_dim(permuted, local_block, 0, keepdims=False)
        block_inv = lax.dynamic_index_in_dim(diag_inv, local_block, 0, keepdims=False)
        summed = lax.psum(partial_value, "col")
        fresh = apply_inverse(own_rhs - summed, block_inv)
        fresh = broadcast(fresh, "row", owner_row)
        first_piece = number * pieces
        offset_piece = (my_col - first_piece) % col_count
        owns = offset_piece < pieces
        which = jnp.clip(offset_piece, 0, pieces - 1)
        local_round = jnp.clip((first_piece + offset_piece) // col_count, 0, rounds - 1)
        piece = lax.dynamic_slice_in_dim(fresh, which * piece_len, piece_len, 1)
        updated = lax.dynamic_update_index_in_dim(solved, piece[:, None, :], local_round, 1)
        return jnp.where(owns, updated, solved)

    start_state = jnp.zeros((rhs_count, rounds, 1, piece_len), jnp.float32)
    return lax.fori_loop(0, total_blocks, advance, start_state)


def solution(mesh):
    return jax.shard_map(
        per_device,
        mesh=mesh,
        in_specs=(P(None, ("row", "col")), P(), P("row", None, "col", None), P("row", None, None)),
        out_specs=P(None, None, "col", None),
        check_vma=False,
    )
```

profile of v0, /device:TPU:0, one launch (start us, length us, event | category | flops | bytes accessed | tf_op | source)
XLA Modules:
  0.0 882.2 jit_solution(17491685887215917001)
XLA Ops:
  9.9 14.1 %gather_fusion = f32[4096,64]{1,0:T(8,128)} fusion(f32[64,4096]{0,1:T(8,128)S(1)} %copy.8, s32[4096]{0:T(1024)S(1)} %fusion.8), kind=kCustom, calls=%fused_computation | custom fusion | bytes 2113536 | tf_op jit(solution)/shard_map/jit(_take)/gather | solution.py:38
  27.4 30.1 %reduce-scatter.2.cloned.1.call-done = f32[2,64,512]{2,1,0:T(8,128)} async-done(((f32[8,64,512]{2,1,0:T(8,128)}), f32[2,64,512]{2,1,0:T(8,128)}) %reduce-scatter.2.cloned.1.call-update) | async-done | bytes 262160 | tf_op jit(solution)/shard_map/reduce_scatter | solution.py:40
  59.3 53.7 %all-reduce.4.cloned.1.call-done = f32[2,64,512]{2,1,0:T(8,128)} async-done(((f32[2,64,512]{2,1,0:T(8,128)}), f32[2,64,512]{2,1,0:T(8,128)}) %all-reduce.4.cloned.1.call-update) | async-done | bytes 262160 | tf_op jit(solution)/shard_map/psum | solution.py:48
  113.0 761.7 %while.16 = (s32[]{:T(128)}, f32[64,4,1,128]{3,1,0,2:T(4,128)S(1)}, s32[]{:T(128)}, f32[2,64,512]{2,1,0:T(8,128)}, f32[1024,512]{1,0:T(8,128)S(1)}, /*index=5*/f...) while((s32[]{:T(128)}, f32[64,4,1,128]{3,1,0,2:T(4,128)S(1)}, ...), condition=%wide.region_5.6_spmd, body=%wide.region_2.5_spmd.sunk | while | flops 402792448 | bytes 4557184 | solution.py:77
  115.0 54.8 %all-reduce.6.cloned.1.call-done = f32[64,512]{1,0:T(8,128)} async-done(((f32[64,512]{1,0:T(8,128)}), f32[64,512]{1,0:T(8,128)}) %all-reduce.6.cloned.1.call-update) | async-done | bytes 131088 | tf_op jit(solution)/shard_map/while/body/eval_jaxpr/psum | solution.py:64
  169.7 3.1 convolution_select_fusion.2
  172.9 34.1 %all-reduce.8.cloned.1.call-done = f32[64,512]{1,0:T(8,128)} async-done(((f32[64,512]{1,0:T(8,128)}), f32[64,512]{1,0:T(8,128)}) %all-reduce.8.cloned.1.call-update) | async-done | bytes 131088 | tf_op jit(solution)/shard_map/while/body/eval_jaxpr/psum | solution.py:9
  210.0 54.8 %all-reduce.6.cloned.1.call-done = f32[64,512]{1,0:T(8,128)} async-done(((f32[64,512]{1,0:T(8,128)}), f32[64,512]{1,0:T(8,128)}) %all-reduce.6.cloned.1.call-update) | async-done | bytes 131088 | tf_op jit(solution)/shard_map/while/body/eval_jaxpr/psum | solution.py:64
  268.0 34.1 %all-reduce.8.cloned.1.call-done = f32[64,512]{1,0:T(8,128)} async-done(((f32[64,512]{1,0:T(8,128)}), f32[64,512]{1,0:T(8,128)}) %all-reduce.8.cloned.1.call-update) | async-done | bytes 131088 | tf_op jit(solution)/shard_map/while/body/eval_jaxpr/psum | solution.py:9
  305.1 55.1 %all-reduce.6.cloned.1.call-done = f32[64,512]{1,0:T(8,128)} async-done(((f32[64,512]{1,0:T(8,128)}), f32[64,512]{1,0:T(8,128)}) %all-reduce.6.cloned.1.call-update) | async-done | bytes 131088 | tf_op jit(solution)/shard_map/while/body/eval_jaxpr/psum | solution.py:64
  363.3 34.1 %all-reduce.8.cloned.1.call-done = f32[64,512]{1,0:T(8,128)} async-done(((f32[64,512]{1,0:T(8,128)}), f32[64,512]{1,0:T(8,128)}) %all-reduce.8.cloned.1.call-update) | async-done | bytes 131088 | tf_op jit(solution)/shard_map/while/body/eval_jaxpr/psum | solution.py:9
  400.4 55.1 %all-reduce.6.cloned.1.call-done = f32[64,512]{1,0:T(8,128)} async-done(((f32[64,512]{1,0:T(8,128)}), f32[64,512]{1,0:T(8,128)}) %all-reduce.6.cloned.1.call-update) | async-done | bytes 131088 | tf_op jit(solution)/shard_map/while/body/eval_jaxpr/psum | solution.py:64
  455.5 3.1 convolution_select_fusion.2
  458.7 34.1 %all-reduce.8.cloned.1.call-done = f32[64,512]{1,0:T(8,128)} async-done(((f32[64,512]{1,0:T(8,128)}), f32[64,512]{1,0:T(8,128)}) %all-reduce.8.cloned.1.call-update) | async-done | bytes 131088 | tf_op jit(solution)/shard_map/while/body/eval_jaxpr/psum | solution.py:9
  495.8 55.1 %all-reduce.6.cloned.1.call-done = f32[64,512]{1,0:T(8,128)} async-done(((f32[64,512]{1,0:T(8,128)}), f32[64,512]{1,0:T(8,128)}) %all-reduce.6.cloned.1.call-update) | async-done | bytes 131088 | tf_op jit(solution)/shard_map/while/body/eval_jaxpr/psum | solution.py:64
  554.1 34.1 %all-reduce.8.cloned.1.call-done = f32[64,512]{1,0:T(8,128)} async-done(((f32[64,512]{1,0:T(8,128)}), f32[64,512]{1,0:T(8,128)}) %all-reduce.8.cloned.1.call-update) | async-done | bytes 131088 | tf_op jit(solution)/shard_map/while/body/eval_jaxpr/psum | solution.py:9
  591.1 55.1 %all-reduce.6.cloned.1.call-done = f32[64,512]{1,0:T(8,128)} async-done(((f32[64,512]{1,0:T(8,128)}), f32[64,512]{1,0:T(8,128)}) %all-reduce.6.cloned.1.call-update) | async-done | bytes 131088 | tf_op jit(solution)/shard_map/while/body/eval_jaxpr/psum | solution.py:64
  646.2 3.1 convolution_select_fusion.2
  649.4 34.1 %all-reduce.8.cloned.1.call-done = f32[64,512]{1,0:T(8,128)} async-done(((f32[64,512]{1,0:T(8,128)}), f32[64,512]{1,0:T(8,128)}) %all-reduce.8.cloned.1.call-update) | async-done | bytes 131088 | tf_op jit(solution)/shard_map/while/body/eval_jaxpr/psum | solution.py:9
  686.5 54.8 %all-reduce.6.cloned.1.call-done = f32[64,512]{1,0:T(8,128)} async-done(((f32[64,512]{1,0:T(8,128)}), f32[64,512]{1,0:T(8,128)}) %all-reduce.6.cloned.1.call-update) | async-done | bytes 131088 | tf_op jit(solution)/shard_map/while/body/eval_jaxpr/psum | solution.py:64
  741.3 3.1 convolution_select_fusion.2
  744.5 34.1 %all-reduce.8.cloned.1.call-done = f32[64,512]{1,0:T(8,128)} async-done(((f32[64,512]{1,0:T(8,128)}), f32[64,512]{1,0:T(8,128)}) %all-reduce.8.cloned.1.call-update) | async-done | bytes 131088 | tf_op jit(solution)/shard_map/while/body/eval_jaxpr/psum | solution.py:9
  781.6 54.8 %all-reduce.6.cloned.1.call-done = f32[64,512]{1,0:T(8,128)} async-done(((f32[64,512]{1,0:T(8,128)}), f32[64,512]{1,0:T(8,128)}) %all-reduce.6.cloned.1.call-update) | async-done | bytes 131088 | tf_op jit(solution)/shard_map/while/body/eval_jaxpr/psum | solution.py:64
  839.5 34.1 %all-reduce.8.cloned.1.call-done = f32[64,512]{1,0:T(8,128)} async-done(((f32[64,512]{1,0:T(8,128)}), f32[64,512]{1,0:T(8,128)}) %all-reduce.8.cloned.1.call-update) | async-done | bytes 131088 | tf_op jit(solution)/shard_map/while/body/eval_jaxpr/psum | solution.py:9
  (83 shorter events, 44.9 us)
Async XLA Ops:
  6.5 51.0 %reduce-scatter.2.cloned.1.call-start = ((), (), s32[]{:S(2)}) async-start(), calls=%async_computation.1 | async-start | bytes 1310720 | tf_op jit(solution)/shard_map/reduce_scatter | solution.py:40
  27.3 85.6 %all-reduce.4.cloned.1.call-start = ((), (), s32[]{:S(2)}) async-start(), calls=%async_computation.2 | async-start | bytes 524288 | tf_op jit(solution)/shard_map/psum | solution.py:48
  113.0 56.7 %all-reduce.6.cloned.1.call-start = ((), (), s32[]{:S(2)}) async-start(), calls=%async_computation.3 | async-start | bytes 262144 | tf_op jit(solution)/shard_map/while/body/eval_jaxpr/psum | solution.py:64
  114.9 92.2 %all-reduce.8.cloned.1.call-start = ((), (), s32[]{:S(2)}) async-start(), calls=%async_computation.4 | async-start | bytes 262144 | tf_op jit(solution)/shard_map/while/body/eval_jaxpr/psum | solution.py:9
  208.1 56.7 %all-reduce.6.cloned.1.call-start = ((), (), s32[]{:S(2)}) async-start(), calls=%async_computation.3 | async-start | bytes 262144 | tf_op jit(solution)/shard_map/while/body/eval_jaxpr/psum | solution.py:64
  209.9 92.2 %all-reduce.8.cloned.1.call-start = ((), (), s32[]{:S(2)}) async-start(), calls=%async_computation.4 | async-start | bytes 262144 | tf_op jit(solution)/shard_map/while/body/eval_jaxpr/psum | solution.py:9
  303.1 57.0 %all-reduce.6.cloned.1.call-start = ((), (), s32[]{:S(2)}) async-start(), calls=%async_computation.3 | async-start | bytes 262144 | tf_op jit(solution)/shard_map/while/body/eval_jaxpr/psum | solution.py:64
  305.0 92.5 %all-reduce.8.cloned.1.call-start = ((), (), s32[]{:S(2)}) async-start(), calls=%async_computation.4 | async-start | bytes 262144 | tf_op jit(solution)/shard_map/while/body/eval_jaxpr/psum | solution.py:9
  398.5 57.0 %all-reduce.6.cloned.1.call-start = ((), (), s32[]{:S(2)}) async-start(), calls=%async_computation.3 | async-start | bytes 262144 | tf_op jit(solution)/shard_map/while/body/eval_jaxpr/psum | solution.py:64
  400.4 92.5 %all-reduce.8.cloned.1.call-start = ((), (), s32[]{:S(2)}) async-start(), calls=%async_computation.4 | async-start | bytes 262144 | tf_op jit(solution)/shard_map/while/body/eval_jaxpr/psum | solution.py:9
  493.8 57.0 %all-reduce.6.cloned.1.call-start = ((), (), s32[]{:S(2)}) async-start(), calls=%async_computation.3 | async-start | bytes 262144 | tf_op jit(solution)/shard_map/while/body/eval_jaxpr/psum | solution.py:64
  495.7 92.5 %all-reduce.8.cloned.1.call-start = ((), (), s32[]{:S(2)}) async-start(), calls=%async_computation.4 | async-start | bytes 262144 | tf_op jit(solution)/shard_map/while/body/eval_jaxpr/psum | solution.py:9
  589.2 57.0 %all-reduce.6.cloned.1.call-start = ((), (), s32[]{:S(2)}) async-start(), calls=%async_computation.3 | async-start | bytes 262144 | tf_op jit(solution)/shard_map/while/body/eval_jaxpr/psum | solution.py:64
  591.1 92.5 %all-reduce.8.cloned.1.call-start = ((), (), s32[]{:S(2)}) async-start(), calls=%async_computation.4 | async-start | bytes 262144 | tf_op jit(solution)/shard_map/while/body/eval_jaxpr/psum | solution.py:9
  684.6 56.7 %all-reduce.6.cloned.1.call-start = ((), (), s32[]{:S(2)}) async-start(), calls=%async_computation.3 | async-start | bytes 262144 | tf_op jit(solution)/shard_map/while/body/eval_jaxpr/psum | solution.py:64
  686.4 92.2 %all-reduce.8.cloned.1.call-start = ((), (), s32[]{:S(2)}) async-start(), calls=%async_computation.4 | async-start | bytes 262144 | tf_op jit(solution)/shard_map/while/body/eval_jaxpr/psum | solution.py:9
  779.6 56.7 %all-reduce.6.cloned.1.call-start = ((), (), s32[]{:S(2)}) async-start(), calls=%async_computation.3 | async-start | bytes 262144 | tf_op jit(solution)/shard_map/while/body/eval_jaxpr/psum | solution.py:64
  781.5 92.2 %all-reduce.8.cloned.1.call-start = ((), (), s32[]{:S(2)}) async-start(), calls=%async_computation.4 | async-start | bytes 262144 | tf_op jit(solution)/shard_map/while/body/eval_jaxpr/psum | solution.py:9
  874.7 0.7 copy-start
Sparse Core Ops, SparseCore 0:
  27.5 29.9 reduce-scatter.1
  60.5 52.3 all-reduce.3
  116.8 52.8 all-reduce.5
  173.0 34.0 all-reduce.7
  211.6 53.1 all-reduce.5
  268.0 34.0 all-reduce.7
  307.0 53.1 all-reduce.5
  363.4 34.0 all-reduce.7
  402.3 53.1 all-reduce.5
  458.8 34.0 all-reduce.7
  497.7 53.1 all-reduce.5
  554.1 34.0 all-reduce.7
  593.0 53.1 all-reduce.5
  649.5 34.0 all-reduce.7
  688.1 53.1 all-reduce.5
  744.6 34.0 all-reduce.7
  783.2 53.1 all-reduce.5
  839.6 34.0 all-reduce.7
where the time goes:
time: 883 us; the launch traced here: 882 us
  waiting for transfers between devices  796 us (90%)
  matrix products  39.5 us (4%)
  local copies, waits for them, and re-layouts  28 us (3%)
  between operations  13.5 us (2%)
    psum x8, waiting for transfers between devices, advance(): summed = lax.psum(partial_value, 'col')  439 us
    psum x8, waiting for transfers between devices, broadcast(): return lax.psum(jnp.where(mine, shard, jnp.zeros_like(shard)), axis)  273 us
    psum x1, waiting for transfers between devices, per_device(): permuted = lax.psum(permuted, 'col')  53.7 us
    reduce_scatter x1, waiting for transfers between devices, per_device(): lax.psum_scatter(jnp.transpose(taken.reshape(rhs_count, blocks_here * lax...  30.1 us
    dot_general x8, matrix products, apply_inverse(): lax.dot_general(values, block_inv, (((1,), (1,)), ((), ())), precision=la...  25.1 us
  transfers between devices with their start and end apart: 18, of which 18 were waited for; matrix products, arithmetic and copies ran while one was open for 0% of the time, Pallas kernels for 0%

commit v1 on v0

--- a/solution.py
+++ b/solution.py
@@ -61,7 +61,7 @@
         )
         own_rhs = lax.dynamic_index_in_dim(permuted, local_block, 0, keepdims=False)
         block_inv = lax.dynamic_index_in_dim(diag_inv, local_block, 0, keepdims=False)
-        summed = lax.psum(partial_value, "col")
+        summed = jnp.sum(lax.all_gather(partial_value, axis_name="col"), 0)
         fresh = apply_inverse(own_rhs - summed, block_inv)
         fresh = broadcast(fresh, "row", owner_row)
         first_piece = number * pieces

time: 883 us -> 648 us (0.73)
  waiting for transfers between devices: 796 us -> 551 us
  other arithmetic: 3 us -> 13.5 us
    psum x8 -> x0, waiting for transfers between devices: 439 us -> none  [advance(): summed = lax.psum(partial_value, 'col')]
    all_gather x0 -> x8, waiting for transfers between devices: none -> 189 us  [advance(): summed = jnp.sum(lax.all_gather(partial_value, axis_name='col'), 0)]
    reduce_sum x0 -> x8, other arithmetic: none -> 10.5 us  [advance(): summed = jnp.sum(lax.all_gather(partial_value, axis_name='col'), 0)]
where the time goes in v1:
time: 648 us; the launch traced here: 647 us
  waiting for transfers between devices  551 us (85%)
  matrix products  38.4 us (6%)
  local copies, waits for them, and re-layouts  28.1 us (4%)
  other arithmetic  13.5 us (2%)
  between operations  13.5 us (2%)
    psum x8, waiting for transfers between devices, broadcast(): return lax.psum(jnp.where(mine, shard, jnp.zeros_like(shard)), axis)  278 us
    all_gather x8, waiting for transfers between devices, advance(): summed = jnp.sum(lax.all_gather(partial_value, axis_name='col'), 0)  189 us
    psum x1, waiting for transfers between devices, per_device(): permuted = lax.psum(permuted, 'col')  53.7 us
    reduce_scatter x1, waiting for transfers between devices, per_device(): lax.psum_scatter(jnp.transpose(taken.reshape(rhs_count, blocks_here * lax...  30.1 us
    dot_general x8, matrix products, apply_inverse(): lax.dot_general(values, block_inv, (((1,), (1,)), ((), ())), precision=la...  23.9 us
    gather x2, local copies, waits for them, and re-layouts, per_device(): taken = jnp.take(rhs, jnp.clip(located, 0, source_len - 1), axis=1)  16.3 us
    dot_general x8, matrix products, advance(): lax.dot_general(solved.reshape(rhs_count, rounds * piece_len), block_rows...  14.4 us
  transfers between devices with their start and end apart: 18, of which 18 were waited for; matrix products, arithmetic and copies ran while one was open for 0% of the time, Pallas kernels for 0%

profile of v1, /device:TPU:0, one launch (start us, length us, event | category | flops | bytes accessed | tf_op | source)
XLA Modules:
  0.0 646.8 jit_solution(2511851599516030363)
XLA Ops:
  9.9 14.2 %gather_fusion = f32[4096,64]{1,0:T(8,128)} fusion(f32[64,4096]{0,1:T(8,128)S(1)} %copy.8, s32[4096]{0:T(1024)S(1)} %fusion.9), kind=kCustom, calls=%fused_computation | custom fusion | bytes 2113536 | tf_op jit(solution)/shard_map/jit(_take)/gather | solution.py:38
  27.5 30.1 %reduce-scatter.2.cloned.1.call-done = f32[2,64,512]{2,1,0:T(8,128)} async-done(((f32[8,64,512]{2,1,0:T(8,128)}), f32[2,64,512]{2,1,0:T(8,128)}) %reduce-scatter.2.cloned.1.call-update) | async-done | bytes 262160 | tf_op jit(solution)/shard_map/reduce_scatter | solution.py:40
  59.4 53.7 %all-reduce.3.cloned.1.call-done = f32[2,64,512]{2,1,0:T(8,128)} async-done(((f32[2,64,512]{2,1,0:T(8,128)}), f32[2,64,512]{2,1,0:T(8,128)}) %all-reduce.3.cloned.1.call-update) | async-done | bytes 262160 | tf_op jit(solution)/shard_map/psum | solution.py:48
  113.1 526.2 %while.16 = (s32[]{:T(128)}, f32[64,4,1,128]{3,1,0,2:T(4,128)S(1)}, s32[]{:T(128)}, f32[2,64,512]{2,1,0:T(8,128)}, f32[1024,512]{1,0:T(8,128)S(1)}, /*index=5*/f...) while((s32[]{:T(128)}, f32[64,4,1,128]{3,1,0,2:T(4,128)S(1)}, ...), condition=%wide.region_5.6_spmd, body=%wide.region_2.5_spmd.sunk | while | flops 402989056 | bytes 9537960 | solution.py:77
  115.1 23.5 %all-gather.5.cloned.1.call-done = f32[512,512]{1,0:T(8,128)} async-done(((f32[64,512]{1,0:T(8,128)}), f32[512,512]{1,0:T(8,128)}) %all-gather.5.cloned.1.call-update) | async-done | bytes 1048592 | tf_op jit(solution)/shard_map/while/body/eval_jaxpr/all_gather | solution.py:64
  143.0 34.7 %all-reduce.5.cloned.1.call-done = f32[64,512]{1,0:T(8,128)} async-done(((f32[64,512]{1,0:T(8,128)}), f32[64,512]{1,0:T(8,128)}) %all-reduce.5.cloned.1.call-update) | async-done | bytes 131088 | tf_op jit(solution)/shard_map/while/body/eval_jaxpr/psum | solution.py:9
  180.7 23.5 %all-gather.5.cloned.1.call-done = f32[512,512]{1,0:T(8,128)} async-done(((f32[64,512]{1,0:T(8,128)}), f32[512,512]{1,0:T(8,128)}) %all-gather.5.cloned.1.call-update) | async-done | bytes 1048592 | tf_op jit(solution)/shard_map/while/body/eval_jaxpr/all_gather | solution.py:64
  208.6 34.7 %all-reduce.5.cloned.1.call-done = f32[64,512]{1,0:T(8,128)} async-done(((f32[64,512]{1,0:T(8,128)}), f32[64,512]{1,0:T(8,128)}) %all-reduce.5.cloned.1.call-update) | async-done | bytes 131088 | tf_op jit(solution)/shard_map/while/body/eval_jaxpr/psum | solution.py:9
  246.3 23.8 %all-gather.5.cloned.1.call-done = f32[512,512]{1,0:T(8,128)} async-done(((f32[64,512]{1,0:T(8,128)}), f32[512,512]{1,0:T(8,128)}) %all-gather.5.cloned.1.call-update) | async-done | bytes 1048592 | tf_op jit(solution)/shard_map/while/body/eval_jaxpr/all_gather | solution.py:64
  274.5 34.7 %all-reduce.5.cloned.1.call-done = f32[64,512]{1,0:T(8,128)} async-done(((f32[64,512]{1,0:T(8,128)}), f32[64,512]{1,0:T(8,128)}) %all-reduce.5.cloned.1.call-update) | async-done | bytes 131088 | tf_op jit(solution)/shard_map/while/body/eval_jaxpr/psum | solution.py:9
  312.2 23.8 %all-gather.5.cloned.1.call-done = f32[512,512]{1,0:T(8,128)} async-done(((f32[64,512]{1,0:T(8,128)}), f32[512,512]{1,0:T(8,128)}) %all-gather.5.cloned.1.call-update) | async-done | bytes 1048592 | tf_op jit(solution)/shard_map/while/body/eval_jaxpr/all_gather | solution.py:64
  337.4 3.0 convolution_select_fusion.2
  340.5 34.7 %all-reduce.5.cloned.1.call-done = f32[64,512]{1,0:T(8,128)} async-done(((f32[64,512]{1,0:T(8,128)}), f32[64,512]{1,0:T(8,128)}) %all-reduce.5.cloned.1.call-update) | async-done | bytes 131088 | tf_op jit(solution)/shard_map/while/body/eval_jaxpr/psum | solution.py:9
  378.2 23.8 %all-gather.5.cloned.1.call-done = f32[512,512]{1,0:T(8,128)} async-done(((f32[64,512]{1,0:T(8,128)}), f32[512,512]{1,0:T(8,128)}) %all-gather.5.cloned.1.call-update) | async-done | bytes 1048592 | tf_op jit(solution)/shard_map/while/body/eval_jaxpr/all_gather | solution.py:64
  403.3 3.0 convolution_select_fusion.2
  406.4 34.7 %all-reduce.5.cloned.1.call-done = f32[64,512]{1,0:T(8,128)} async-done(((f32[64,512]{1,0:T(8,128)}), f32[64,512]{1,0:T(8,128)}) %all-reduce.5.cloned.1.call-update) | async-done | bytes 131088 | tf_op jit(solution)/shard_map/while/body/eval_jaxpr/psum | solution.py:9
  444.1 23.8 %all-gather.5.cloned.1.call-done = f32[512,512]{1,0:T(8,128)} async-done(((f32[64,512]{1,0:T(8,128)}), f32[512,512]{1,0:T(8,128)}) %all-gather.5.cloned.1.call-update) | async-done | bytes 1048592 | tf_op jit(solution)/shard_map/while/body/eval_jaxpr/all_gather | solution.py:64
  472.3 34.7 %all-reduce.5.cloned.1.call-done = f32[64,512]{1,0:T(8,128)} async-done(((f32[64,512]{1,0:T(8,128)}), f32[64,512]{1,0:T(8,128)}) %all-reduce.5.cloned.1.call-update) | async-done | bytes 131088 | tf_op jit(solution)/shard_map/while/body/eval_jaxpr/psum | solution.py:9
  510.0 23.5 %all-gather.5.cloned.1.call-done = f32[512,512]{1,0:T(8,128)} async-done(((f32[64,512]{1,0:T(8,128)}), f32[512,512]{1,0:T(8,128)}) %all-gather.5.cloned.1.call-update) | async-done | bytes 1048592 | tf_op jit(solution)/shard_map/while/body/eval_jaxpr/all_gather | solution.py:64
  534.9 3.0 convolution_select_fusion.2
  537.9 34.7 %all-reduce.5.cloned.1.call-done = f32[64,512]{1,0:T(8,128)} async-done(((f32[64,512]{1,0:T(8,128)}), f32[64,512]{1,0:T(8,128)}) %all-reduce.5.cloned.1.call-update) | async-done | bytes 131088 | tf_op jit(solution)/shard_map/while/body/eval_jaxpr/psum | solution.py:9
  575.7 23.5 %all-gather.5.cloned.1.call-done = f32[512,512]{1,0:T(8,128)} async-done(((f32[64,512]{1,0:T(8,128)}), f32[512,512]{1,0:T(8,128)}) %all-gather.5.cloned.1.call-update) | async-done | bytes 1048592 | tf_op jit(solution)/shard_map/while/body/eval_jaxpr/all_gather | solution.py:64
  600.5 3.0 convolution_select_fusion.2
  603.6 34.7 %all-reduce.5.cloned.1.call-done = f32[64,512]{1,0:T(8,128)} async-done(((f32[64,512]{1,0:T(8,128)}), f32[64,512]{1,0:T(8,128)}) %all-reduce.5.cloned.1.call-update) | async-done | bytes 131088 | tf_op jit(solution)/shard_map/while/body/eval_jaxpr/psum | solution.py:9
  (107 shorter events, 54.8 us)
Async XLA Ops:
  6.5 51.1 %reduce-scatter.2.cloned.1.call-start = ((), (), s32[]{:S(2)}) async-start(), calls=%async_computation.1 | async-start | bytes 1310720 | tf_op jit(solution)/shard_map/reduce_scatter | solution.py:40
  27.4 85.6 %all-reduce.3.cloned.1.call-start = ((), (), s32[]{:S(2)}) async-start(), calls=%async_computation.2 | async-start | bytes 524288 | tf_op jit(solution)/shard_map/psum | solution.py:48
  113.1 26.8 %copy-start.1 = (f32[2,64,512]{2,1,0:T(8,128)S(1)}, f32[2,64,512]{2,1,0:T(8,128)}, u32[]{:S(2)}) copy-start(f32[2,64,512]{2,1,0:T(8,128)} %get-tuple-element.288) | copy-start | bytes 786436 | tf_op jit(solution)/shard_map/while
  113.1 25.5 %all-gather.5.cloned.1.call-start = ((), (), s32[]{:S(2)}) async-start(), calls=%async_computation.3 | async-start | bytes 1179648 | tf_op jit(solution)/shard_map/while/body/eval_jaxpr/all_gather | solution.py:64
  115.0 62.7 %all-reduce.5.cloned.1.call-start = ((), (), s32[]{:S(2)}) async-start(), calls=%async_computation.4 | async-start | bytes 262144 | tf_op jit(solution)/shard_map/while/body/eval_jaxpr/psum | solution.py:9
  178.7 25.5 %all-gather.5.cloned.1.call-start = ((), (), s32[]{:S(2)}) async-start(), calls=%async_computation.3 | async-start | bytes 1179648 | tf_op jit(solution)/shard_map/while/body/eval_jaxpr/all_gather | solution.py:64
  180.6 62.7 %all-reduce.5.cloned.1.call-start = ((), (), s32[]{:S(2)}) async-start(), calls=%async_computation.4 | async-start | bytes 262144 | tf_op jit(solution)/shard_map/while/body/eval_jaxpr/psum | solution.py:9
  244.3 27.1 %copy-start.1 = (f32[2,64,512]{2,1,0:T(8,128)S(1)}, f32[2,64,512]{2,1,0:T(8,128)}, u32[]{:S(2)}) copy-start(f32[2,64,512]{2,1,0:T(8,128)} %get-tuple-element.288) | copy-start | bytes 786436 | tf_op jit(solution)/shard_map/while
  244.4 25.8 %all-gather.5.cloned.1.call-start = ((), (), s32[]{:S(2)}) async-start(), calls=%async_computation.3 | async-start | bytes 1179648 | tf_op jit(solution)/shard_map/while/body/eval_jaxpr/all_gather | solution.py:64
  246.2 63.0 %all-reduce.5.cloned.1.call-start = ((), (), s32[]{:S(2)}) async-start(), calls=%async_computation.4 | async-start | bytes 262144 | tf_op jit(solution)/shard_map/while/body/eval_jaxpr/psum | solution.py:9
  310.3 27.1 %copy-start.1 = (f32[2,64,512]{2,1,0:T(8,128)S(1)}, f32[2,64,512]{2,1,0:T(8,128)}, u32[]{:S(2)}) copy-start(f32[2,64,512]{2,1,0:T(8,128)} %get-tuple-element.288) | copy-start | bytes 786436 | tf_op jit(solution)/shard_map/while
  310.3 25.8 %all-gather.5.cloned.1.call-start = ((), (), s32[]{:S(2)}) async-start(), calls=%async_computation.3 | async-start | bytes 1179648 | tf_op jit(solution)/shard_map/while/body/eval_jaxpr/all_gather | solution.py:64
  312.2 63.0 %all-reduce.5.cloned.1.call-start = ((), (), s32[]{:S(2)}) async-start(), calls=%async_computation.4 | async-start | bytes 262144 | tf_op jit(solution)/shard_map/while/body/eval_jaxpr/psum | solution.py:9
  376.2 27.1 %copy-start.1 = (f32[2,64,512]{2,1,0:T(8,128)S(1)}, f32[2,64,512]{2,1,0:T(8,128)}, u32[]{:S(2)}) copy-start(f32[2,64,512]{2,1,0:T(8,128)} %get-tuple-element.288) | copy-start | bytes 786436 | tf_op jit(solution)/shard_map/while
  376.2 25.8 %all-gather.5.cloned.1.call-start = ((), (), s32[]{:S(2)}) async-start(), calls=%async_computation.3 | async-start | bytes 1179648 | tf_op jit(solution)/shard_map/while/body/eval_jaxpr/all_gather | solution.py:64
  378.1 63.0 %all-reduce.5.cloned.1.call-start = ((), (), s32[]{:S(2)}) async-start(), calls=%async_computation.4 | async-start | bytes 262144 | tf_op jit(solution)/shard_map/while/body/eval_jaxpr/psum | solution.py:9
  442.1 27.1 %copy-start.1 = (f32[2,64,512]{2,1,0:T(8,128)S(1)}, f32[2,64,512]{2,1,0:T(8,128)}, u32[]{:S(2)}) copy-start(f32[2,64,512]{2,1,0:T(8,128)} %get-tuple-element.288) | copy-start | bytes 786436 | tf_op jit(solution)/shard_map/while
  442.1 25.8 %all-gather.5.cloned.1.call-start = ((), (), s32[]{:S(2)}) async-start(), calls=%async_computation.3 | async-start | bytes 1179648 | tf_op jit(solution)/shard_map/while/body/eval_jaxpr/all_gather | solution.py:64
  444.0 63.0 %all-reduce.5.cloned.1.call-start = ((), (), s32[]{:S(2)}) async-start(), calls=%async_computation.4 | async-start | bytes 262144 | tf_op jit(solution)/shard_map/while/body/eval_jaxpr/psum | solution.py:9
  508.1 26.8 %copy-start.1 = (f32[2,64,512]{2,1,0:T(8,128)S(1)}, f32[2,64,512]{2,1,0:T(8,128)}, u32[]{:S(2)}) copy-start(f32[2,64,512]{2,1,0:T(8,128)} %get-tuple-element.288) | copy-start | bytes 786436 | tf_op jit(solution)/shard_map/while
  508.1 25.5 %all-gather.5.cloned.1.call-start = ((), (), s32[]{:S(2)}) async-start(), calls=%async_computation.3 | async-start | bytes 1179648 | tf_op jit(solution)/shard_map/while/body/eval_jaxpr/all_gather | solution.py:64
  510.0 62.7 %all-reduce.5.cloned.1.call-start = ((), (), s32[]{:S(2)}) async-start(), calls=%async_computation.4 | async-start | bytes 262144 | tf_op jit(solution)/shard_map/while/body/eval_jaxpr/psum | solution.py:9
  573.7 25.5 %all-gather.5.cloned.1.call-start = ((), (), s32[]{:S(2)}) async-start(), calls=%async_computation.3 | async-start | bytes 1179648 | tf_op jit(solution)/shard_map/while/body/eval_jaxpr/all_gather | solution.py:64
  575.6 62.7 %all-reduce.5.cloned.1.call-start = ((), (), s32[]{:S(2)}) async-start(), calls=%async_computation.4 | async-start | bytes 262144 | tf_op jit(solution)/shard_map/while/body/eval_jaxpr/psum | solution.py:9
  (3 other events, 54.3 us)
Sparse Core Ops, SparseCore 0:
  27.6 29.9 reduce-scatter.1
  60.6 52.3 all-reduce.2
  115.8 22.7 all-gather.4
  143.1 34.6 all-reduce.4
  181.1 23.0 all-gather.4
  208.7 34.6 all-reduce.4
  247.1 23.0 all-gather.4
  274.6 34.6 all-reduce.4
  313.0 23.0 all-gather.4
  340.5 34.6 all-reduce.4
  378.9 23.0 all-gather.4
  406.5 34.6 all-reduce.4
  444.9 23.0 all-gather.4
  472.4 34.6 all-reduce.4
  510.5 23.0 all-gather.4
  538.0 34.6 all-reduce.4
  576.1 23.0 all-gather.4
  603.6 34.6 all-reduce.4
